TPU v7x, 32 devices: a whole 2x2x4 slice. The times are simulated.
32 devices in a mesh: wide: 8 (over y, x, core), narrow: 4 (over z).
Axes of the slice: x: 2, y: 2, z: 4, core: 2. Of those that a mesh axis runs over, the one named last changes fastest.
Arguments:
- layer_input: bfloat16 [4, 2048, 2048], P(None, 'wide'), may hold values from -6 to 6
- grad_out: bfloat16 [4, 2048, 2048], P(None, 'wide'), may hold values from -6 to 6
- lengths: int32 [4, 8], replicated, may hold values from 1 to 1024, 2048 in all within a row
- w_query: bfloat16 [2048, 2048], P('wide', 'narrow'), may hold values from -0.125 to 0.125
- w_key: bfloat16 [2048, 1024], P('wide', 'narrow'), may hold values from -0.125 to 0.125
- w_value: bfloat16 [2048, 1024], P('wide', 'narrow'), may hold values from -0.125 to 0.125
- w_out: bfloat16 [2048, 2048], P('narrow', 'wide'), may hold values from -0.75 to 0.75
- w_gate: bfloat16 [2048, 6144], P('wide', 'narrow'), may hold values from -0.125 to 0.125
- w_up: bfloat16 [2048, 6144], P('wide', 'narrow'), may hold values from -0.125 to 0.125
- w_down: bfloat16 [6144, 2048], P('narrow', 'wide'), may hold values from -0.078125 to 0.078125
- gain_attn: float32 [2048], replicated, may hold values from 0.25 to 1.75
- gain_ffn: float32 [2048], replicated, may hold values from 0.25 to 1.75
- gain_query: float32 [128], replicated, may hold values from 0.25 to 1.75
- gain_key: float32 [128], replicated, may hold values from 0.25 to 1.75
Outputs:
- output: bfloat16 [4, 2048, 2048], P(None, 'wide')
- grad_input: float32 [4, 2048, 2048], P(None, 'wide')
- grad_wquery: float32 [2048, 2048], P('wide', 'narrow')
- grad_wkey: float32 [2048, 1024], P('wide', 'narrow')
- grad_wvalue: float32 [2048, 1024], P('wide', 'narrow')
- grad_wout: float32 [2048, 2048], P('narrow', 'wide')
- grad_wgate: float32 [2048, 6144], P('wide', 'narrow')
- grad_wup: float32 [2048, 6144], P('wide', 'narrow')
- grad_wdown: float32 [6144, 2048], P('narrow', 'wide')
- grad_gattn: float32 [2048], replicated
- grad_gffn: float32 [2048], replicated
- grad_gquery: float32 [128], replicated
- grad_gkey: float32 [128], replicated
Inputs may be any that keep to these rules, and one draw needn't show every extreme that they name: `lengths`: each row cuts the 2048 tokens of its micro-batch into 8 consecutive pieces in order; pieces 0 to 6 are documents and the last piece is padding. A row's pieces sum to 2048, and its largest piece is exactly 1024.
All inputs are finite; a program needn't handle non-finite values.
Results may differ from a plain program's by a relative error of at most 0.022.
Values may be sent and summed in bfloat16 or wider, within the bound.
A program may use at most 256 MiB of HBM per device.

v0:
```python
import math
import jax
import jax.numpy as jnp
from jax import lax
from jax.sharding import PartitionSpec as P

HD = 128
NDOC = 8
EPSILON = 1e-06
THETA = 1000000.0


def rms_norm(values, gain):
    return values * lax.rsqrt(jnp.mean(values * values, axis=-1, keepdims=True) + EPSILON) * gain


def unit_rows(values):
    return values * lax.rsqrt(jnp.mean(values * values, axis=-1, keepdims=True) + EPSILON)


def rotate(values, cosine, sine):
    midway = values.shape[-1] // 2
    turned = jnp.concatenate([-values[..., midway:], values[..., :midway]], axis=-1)
    return values * cosine + turned * sine


def layout(lengths_row, total):
    finish = jnp.cumsum(lengths_row)
    starts = finish - lengths_row
    places = jnp.arange(total, dtype=jnp.int32)
    segment = jnp.sum((places[:, None] >= finish[None, :]).astype(jnp.int32), axis=1)
    member = segment[:, None] == jnp.arange(finish.shape[0], dtype=jnp.int32)[None, :]
    opening = jnp.sum(jnp.where(member, starts[None, :], 0), axis=1)
    return (segment, places - opening)


def angles(place):
    frequency = jnp.exp(-math.log(THETA) * jnp.arange(0, HD, 2).astype(jnp.float32) / HD)
    turning = place.astype(jnp.float32)[:, None] * frequency[None, :]
    turning = jnp.concatenate([turning, turning], axis=-1)
    return (jnp.cos(turning), jnp.sin(turning))


def allowed(query_seg, query_idx, key_seg, key_idx):
    same_doc = query_seg[:, None] == key_seg[None, :]
    causal = key_idx[None, :] <= query_idx[:, None]
    usable = (key_seg[None, :] != NDOC - 1) | (key_idx[None, :] == query_idx[:, None])
    return same_doc & causal & usable


def attention_scores(query_low, key_all, mask_local, factor):
    scores = (
        jnp.einsum("tgrd,kgd->grtk", query_low, key_all, preferred_element_type=jnp.float32)
        * factor
    )
    return jnp.where(mask_local[None, None], scores, -1e30)


def one_batch(row_input, grad_row, lengths_row, gathered, gains):
    w_query, w_key, w_value, w_out, w_gate, w_up, w_down = gathered
    gain_attn, gain_ffn, gain_query, gain_key = gains
    tok_rows = row_input.shape[0]
    total = tok_rows * lax.axis_size("wide")
    groups = w_key.shape[1] // HD
    repeat = w_query.shape[1] // w_key.shape[1]
    factor = 1.0 / math.sqrt(HD)
    first_row = lax.axis_index("wide") * tok_rows
    segment, place = layout(lengths_row, total)
    positions = jnp.arange(total, dtype=jnp.int32)
    query_seg = lax.dynamic_slice_in_dim(segment, first_row, tok_rows)
    query_idx = lax.dynamic_slice_in_dim(positions, first_row, tok_rows)
    mask_local = allowed(query_seg, query_idx, segment, positions)
    cosine, sine = angles(lax.dynamic_slice_in_dim(place, first_row, tok_rows))

    def head_norm(rows, gain):
        return rotate(rms_norm(rows, gain), cosine[:, None, :], sine[:, None, :])

    input_float = row_input.astype(jnp.float32)
    grad_float = grad_row.astype(jnp.float32)
    normed_one, pull_one = jax.vjp(lambda rows: rms_norm(rows, gain_attn), input_float)
    hidden_one = normed_one.astype(jnp.bfloat16)
    query_raw = jnp.dot(hidden_one, w_query, preferred_element_type=jnp.float32).reshape(
        tok_rows, groups * repeat, HD
    )
    key_raw = jnp.dot(hidden_one, w_key, preferred_element_type=jnp.float32).reshape(
        tok_rows, groups, HD
    )
    value_low = jnp.dot(hidden_one, w_value, preferred_element_type=jnp.float32).astype(
        jnp.bfloat16
    )
    query_turned, pull_query = jax.vjp(head_norm, query_raw, gain_query)
    key_turned, pull_key = jax.vjp(head_norm, key_raw, gain_key)
    query_low = query_turned.astype(jnp.bfloat16).reshape(tok_rows, groups, repeat, HD)
    key_low = key_turned.astype(jnp.bfloat16).reshape(tok_rows, groups * HD)
    key_all, value_all = (
        lax.all_gather(key_low, "wide", axis=0, tiled=True),
        lax.all_gather(value_low, "wide", axis=0, tiled=True),
    )
    key_all = key_all.reshape(total, groups, HD)
    value_all = value_all.reshape(total, groups, HD)
    scores = attention_scores(query_low, key_all, mask_local, factor)
    highest = jnp.max(scores, axis=-1, keepdims=True)
    exponent = jnp.exp(scores - highest)
    denominator = jnp.sum(exponent, axis=-1, keepdims=True)
    log_total = highest + jnp.log(denominator)
    probs_low = (exponent / denominator).astype(jnp.bfloat16)
    mixed = jnp.einsum("grtk,kgd->tgrd", probs_low, value_all, preferred_element_type=jnp.float32)
    mixed_low = mixed.reshape(tok_rows, groups * repeat * HD).astype(jnp.bfloat16)
    attn_part = jnp.dot(mixed_low, w_out, preferred_element_type=jnp.float32)
    middle = input_float + lax.psum(attn_part.astype(jnp.bfloat16), "narrow").astype(jnp.float32)
    normed_two, pull_two = jax.vjp(lambda rows: rms_norm(rows, gain_ffn), middle)
    hidden_two = normed_two.astype(jnp.bfloat16)
    unit_two = unit_rows(middle)
    gate = jnp.dot(hidden_two, w_gate, preferred_element_type=jnp.float32)
    up_proj = jnp.dot(hidden_two, w_up, preferred_element_type=jnp.float32)
    active, pull_active = jax.vjp(
        lambda gate_in, up_in: jax.nn.silu(gate_in) * up_in, gate, up_proj
    )
    active_low = active.astype(jnp.bfloat16)
    ffn_part = jnp.dot(active_low, w_down, preferred_element_type=jnp.float32)
    output_low = (
        middle + lax.psum(ffn_part.astype(jnp.bfloat16), "narrow").astype(jnp.float32)
    ).astype(jnp.bfloat16)
    grad_wdown = jnp.einsum("tf,td->fd", active_low, grad_row, preferred_element_type=jnp.float32)
    grad_active = jnp.einsum("td,fd->tf", grad_row, w_down, preferred_element_type=jnp.float32)
    grad_gate, grad_upper = pull_active(grad_active)
    gate_back = grad_gate.astype(jnp.bfloat16)
    upper_back = grad_upper.astype(jnp.bfloat16)
    grad_wgate = jnp.einsum("td,tf->df", hidden_two, gate_back, preferred_element_type=jnp.float32)
    grad_wup = jnp.einsum("td,tf->df", hidden_two, upper_back, preferred_element_type=jnp.float32)
    partial_two = jnp.einsum(
        "tf,df->td", gate_back, w_gate, preferred_element_type=jnp.float32
    ) + jnp.einsum("tf,df->td", upper_back, w_up, preferred_element_type=jnp.float32)
    gain_two = jnp.sum(partial_two * unit_two, axis=0)
    grad_middle = (
        grad_float
        + pull_two(lax.psum(partial_two.astype(jnp.bfloat16), "narrow").astype(jnp.float32))[0]
    )
    middle_low = grad_middle.astype(jnp.bfloat16)
    grad_wout = jnp.einsum("th,td->hd", mixed_low, middle_low, preferred_element_type=jnp.float32)
    grad_mixed = jnp.einsum("td,hd->th", middle_low, w_out, preferred_element_type=jnp.float32)
    grad_mixed = grad_mixed.astype(jnp.bfloat16).reshape(tok_rows, groups, repeat, HD)
    scores = attention_scores(query_low, key_all, mask_local, factor)
    probs = jnp.exp(scores - log_total)
    grad_probs = jnp.einsum(
        "tgrd,kgd->grtk", grad_mixed, value_all, preferred_element_type=jnp.float32
    )
    weighted = jnp.sum(probs * grad_probs, axis=-1, keepdims=True)
    grad_scores = (probs * (grad_probs - weighted)).astype(jnp.bfloat16)
    grad_turned = (
        jnp.einsum("grtk,kgd->tgrd", grad_scores, key_all, preferred_element_type=jnp.float32)
        * factor
    )
    grad_keyall = (
        jnp.einsum("grtk,tgrd->kgd", grad_scores, query_low, preferred_element_type=jnp.float32)
        * factor
    )
    grad_valueall = jnp.einsum(
        "grtk,tgrd->kgd", probs.astype(jnp.bfloat16), grad_mixed, preferred_element_type=jnp.float32
    )
    grad_keys, grad_values = (
        lax.psum_scatter(
            grad_keyall.reshape(total, groups * HD).astype(jnp.bfloat16),
            "wide",
            scatter_dimension=0,
            tiled=True,
        ).astype(jnp.float32),
        lax.psum_scatter(
            grad_valueall.reshape(total, groups * HD).astype(jnp.bfloat16),
            "wide",
            scatter_dimension=0,
            tiled=True,
        ).astype(jnp.float32),
    )
    grad_qraw, gain_q = pull_query(grad_turned.reshape(tok_rows, groups * repeat, HD))
    grad_kraw, gain_k = pull_key(grad_keys.reshape(tok_rows, groups, HD))
    query_back = grad_qraw.reshape(tok_rows, groups * repeat * HD).astype(jnp.bfloat16)
    key_back = grad_kraw.reshape(tok_rows, groups * HD).astype(jnp.bfloat16)
    value_back = grad_values.astype(jnp.bfloat16)
    grad_wquery = jnp.einsum(
        "td,th->dh", hidden_one, query_back, preferred_element_type=jnp.float32
    )
    grad_wkey = jnp.einsum("td,th->dh", hidden_one, key_back, preferred_element_type=jnp.float32)
    grad_wvalue = jnp.einsum(
        "td,th->dh", hidden_one, value_back, preferred_element_type=jnp.float32
    )
    partial_one = (
        jnp.einsum("th,dh->td", query_back, w_query, preferred_element_type=jnp.float32)
        + jnp.einsum("th,dh->td", key_back, w_key, preferred_element_type=jnp.float32)
        + jnp.einsum("th,dh->td", value_back, w_value, preferred_element_type=jnp.float32)
    )
    gain_one = jnp.sum(partial_one * unit_rows(input_float), axis=0)
    grad_input = (
        grad_middle
        + pull_one(lax.psum(partial_one.astype(jnp.bfloat16), "narrow").astype(jnp.float32))[0]
    )
    weight_grads = (
        grad_wquery,
        grad_wkey,
        grad_wvalue,
        grad_wout,
        grad_wgate,
        grad_wup,
        grad_wdown,
    )
    return (output_low, grad_input, weight_grads, (gain_one, gain_two, gain_q, gain_k))


def local(
    layer_input,
    grad_out,
    lengths,
    w_query,
    w_key,
    w_value,
    w_out,
    w_gate,
    w_up,
    w_down,
    gain_attn,
    gain_ffn,
    gain_query,
    gain_key,
):
    width = lax.axis_size("wide")
    shards = (w_query, w_key, w_value, w_out, w_gate, w_up, w_down)
    along_rows = (True, True, True, False, True, True, False)
    gains = (gain_attn, gain_ffn, gain_query, gain_key)
    totals = tuple(
        (
            jnp.zeros(
                (
                    (piece.shape[0] * width, piece.shape[1])
                    if rows_first
                    else (piece.shape[0], piece.shape[1] * width)
                ),
                jnp.float32,
            )
            for piece, rows_first in zip(shards, along_rows)
        )
    )
    gain_terms = tuple((jnp.zeros(gain.shape, jnp.float32) for gain in gains))
    outputs = []
    grad_inputs = []
    for micro in range(layer_input.shape[0]):
        gathered = (
            lax.all_gather(w_query, "wide", axis=0, tiled=True),
            lax.all_gather(w_key, "wide", axis=0, tiled=True),
            lax.all_gather(w_value, "wide", axis=0, tiled=True),
            lax.all_gather(w_out, "wide", axis=1, tiled=True),
            lax.all_gather(w_gate, "wide", axis=0, tiled=True),
            lax.all_gather(w_up, "wide", axis=0, tiled=True),
            lax.all_gather(w_down, "wide", axis=1, tiled=True),
        )
        output, grad_input, weight_grads, gain_grads = one_batch(
            layer_input[micro], grad_out[micro], lengths[micro], gathered, gains
        )
        outputs.append(output)
        grad_inputs.append(grad_input)
        gain_terms = tuple((running + fresh for running, fresh in zip(gain_terms, gain_grads)))
        totals = tuple((running + fresh for running, fresh in zip(totals, weight_grads)))
    results = (
        lax.psum_scatter(
            totals[0].astype(jnp.bfloat16), "wide", scatter_dimension=0, tiled=True
        ).astype(jnp.float32),
        lax.psum_scatter(
            totals[1].astype(jnp.bfloat16), "wide", scatter_dimension=0, tiled=True
        ).astype(jnp.float32),
        lax.psum_scatter(
            totals[2].astype(jnp.bfloat16), "wide", scatter_dimension=0, tiled=True
        ).astype(jnp.float32),
        lax.psum_scatter(
            totals[3].astype(jnp.bfloat16), "wide", scatter_dimension=1, tiled=True
        ).astype(jnp.float32),
        lax.psum_scatter(
            totals[4].astype(jnp.bfloat16), "wide", scatter_dimension=0, tiled=True
        ).astype(jnp.float32),
        lax.psum_scatter(
            totals[5].astype(jnp.bfloat16), "wide", scatter_dimension=0, tiled=True
        ).astype(jnp.float32),
        lax.psum_scatter(
            totals[6].astype(jnp.bfloat16), "wide", scatter_dimension=1, tiled=True
        ).astype(jnp.float32),
    )
    gain_total = lax.psum(gain_terms, ("wide", "narrow"))
    return (
        jnp.stack(outputs),
        jnp.stack(grad_inputs),
        results[0],
        results[1],
        results[2],
        results[3],
        results[4],
        results[5],
        results[6],
        gain_total[0],
        gain_total[1],
        gain_total[2],
        gain_total[3],
    )


def solution(mesh):
    in_specs = (
        P(None, "wide", None),
        P(None, "wide", None),
        P(),
        P("wide", "narrow"),
        P("wide", "narrow"),
        P("wide", "narrow"),
        P("narrow", "wide"),
        P("wide", "narrow"),
        P("wide", "narrow"),
        P("narrow", "wide"),
        P(),
        P(),
        P(),
        P(),
    )
    out_specs = (
        P(None, "wide", None),
        P(None, "wide", None),
        P("wide", "narrow"),
        P("wide", "narrow"),
        P("wide", "narrow"),
        P("narrow", "wide"),
        P("wide", "narrow"),
        P("wide", "narrow"),
        P("narrow", "wide"),
        P(),
        P(),
        P(),
        P(),
    )
    return jax.shard_map(local, mesh=mesh, in_specs=in_specs, out_specs=out_specs, check_vma=False)
```

profile of v0, /device:TPU:0, one launch (start us, length us, event | category | flops | bytes accessed | tf_op | source)
XLA Modules:
  0.0 1960.0 jit_solution(11782084816646856816)
XLA Ops:
  14.2 21.9 %all-gather.16.cloned.1.call-done = bf16[2048,256]{1,0:T(8,128)(2,1)} async-done(((bf16[256,256]{1,0:T(8,128)(2,1)}), bf16[2048,256]{1,0:T(8,128)(2,1)}) %all-gather.16.cloned.1.call-update) | async-done | bytes 1048592 | tf_op jit(solution)/shard_map/all_gather | solution.py:249
  39.5 21.8 %all-gather.20.cloned.1.call-done = bf16[2048,256]{1,0:T(8,128)(2,1)} async-done(((bf16[256,256]{1,0:T(8,128)(2,1)}), bf16[2048,256]{1,0:T(8,128)(2,1)}) %all-gather.20.cloned.1.call-update) | async-done | bytes 1048592 | tf_op jit(solution)/shard_map/all_gather | solution.py:248
  72.1 18.9 all-gather.24.cloned.1.call-done
  94.9 21.8 %all-gather.38.cloned.1.call-done = bf16[2048,256]{1,0:T(8,128)(2,1)} async-done(((bf16[256,256]{1,0:T(8,128)(2,1)}), bf16[2048,256]{1,0:T(8,128)(2,1)}) %all-gather.38.cloned.1.call-update) | async-done | bytes 1048592 | tf_op jit(solution)/shard_map/all_gather | solution.py:97
  122.2 20.3 %all-gather.40.cloned.1.call-done = bf16[2048,256]{0,1:T(8,128)(2,1)} async-done(((bf16[256,256]{0,1:T(8,128)(2,1)}), bf16[2048,256]{0,1:T(8,128)(2,1)}) %all-gather.40.cloned.1.call-update) | async-done | bytes 1048592 | tf_op jit(solution)/shard_map/all_gather | solution.py:96
  150.4 22.0 %all-gather.26.cloned.1.call-done = bf16[512,2048]{1,0:T(8,128)(2,1)} async-done(((bf16[512,256]{1,0:T(8,128)(2,1)}), bf16[512,2048]{1,0:T(8,128)(2,1)}) %all-gather.26.cloned.1.call-update) | async-done | bytes 2097168 | tf_op jit(solution)/shard_map/all_gather | solution.py:250
  175.8 52.0 %all-reduce.25.cloned.1.call-done = bf16[256,2048]{1,0:T(8,128)(2,1)} async-done(((bf16[256,2048]{1,0:T(8,128)(2,1)}), bf16[256,2048]{1,0:T(8,128)(2,1)}) %all-reduce.25.cloned.1.call-update) | async-done | bytes 1048592 | tf_op jit(solution)/shard_map/psum | solution.py:110
  262.1 20.4 %all-gather.18.cloned.1.call-done = bf16[2048,256]{1,0:T(8,128)(2,1)} async-done(((bf16[256,256]{1,0:T(8,128)(2,1)}), bf16[2048,256]{1,0:T(8,128)(2,1)}) %all-gather.18.cloned.1.call-update) | async-done | bytes 1048592 | tf_op jit(solution)/shard_map/all_gather | solution.py:97
  284.6 23.5 %all-gather.34.cloned.1.call-done = bf16[2048,256]{1,0:T(8,128)(2,1)} async-done(((bf16[256,256]{1,0:T(8,128)(2,1)}), bf16[2048,256]{1,0:T(8,128)(2,1)}) %all-gather.34.cloned.1.call-update) | async-done | bytes 1048592 | tf_op jit(solution)/shard_map/all_gather | solution.py:97
  310.5 23.6 %all-gather.44.cloned.1.call-done = bf16[2048,256]{0,1:T(8,128)(2,1)} async-done(((bf16[256,256]{0,1:T(8,128)(2,1)}), bf16[2048,256]{0,1:T(8,128)(2,1)}) %all-gather.44.cloned.1.call-update) | async-done | bytes 1048592 | tf_op jit(solution)/shard_map/all_gather | solution.py:96
  344.3 15.1 all-gather.22.cloned.1.call-done
  369.8 15.0 all-gather.36.cloned.1.call-done
  395.0 36.9 %all-gather.28.cloned.1.call-done = bf16[2048,1536]{1,0:T(8,128)(2,1)} async-done(((bf16[256,1536]{1,0:T(8,128)(2,1)}), bf16[2048,1536]{1,0:T(8,128)(2,1)}) %all-gather.28.cloned.1.call-update) | async-done | bytes 6291472 | tf_op jit(solution)/shard_map/all_gather | solution.py:251
  431.9 5.7 fusion.381
  437.6 42.6 %all-gather.32.cloned.1.call-done = bf16[1536,2048]{1,0:T(8,128)(2,1)} async-done(((bf16[1536,256]{1,0:T(8,128)(2,1)}), bf16[1536,2048]{1,0:T(8,128)(2,1)}) %all-gather.32.cloned.1.call-update) | async-done | bytes 6291472 | tf_op jit(solution)/shard_map/all_gather | solution.py:253
  480.2 6.1 fusion.179
  486.3 41.1 %all-gather.30.cloned.1.call-done = bf16[2048,1536]{1,0:T(8,128)(2,1)} async-done(((bf16[256,1536]{1,0:T(8,128)(2,1)}), bf16[2048,1536]{1,0:T(8,128)(2,1)}) %all-gather.30.cloned.1.call-update) | async-done | bytes 6291472 | tf_op jit(solution)/shard_map/all_gather | solution.py:252
  527.4 6.8 multiply_convert_fusion.9
  534.2 5.2 fusion.390
  543.0 155.1 %all-reduce.31.cloned.1.call-done = (bf16[256,2048]{1,0:T(8,128)(2,1)}, bf16[256,2048]{1,0:T(8,128)(2,1)}, bf16[256,2048]{1,0:T(8,128)(2,1)}, bf16[256,2048]{1,0:T(8,128)(2,1)}) async-done(((bf16[256,2048]{1,0:T(8,128)(2,1)}, bf16[256,2048]{1,0:T(8,128)(2,1)}, bf16[256,2048]{1,0:T(8,128)(2,1)}, bf16[256,2048]{1,0:T(8,128)(2,1)}), (bf16[256,2048]{1,0:T(8,128)(2,1)}, bf16[256,2048]{1,0:T(8,128)(2,1)}, ...) | async-done | bytes 4194320 | tf_op jit(solution)/shard_map/psum | solution.py:110
  698.2 6.1 multiply_reduce_fusion.1
  706.5 6.9 fusion.382
  733.9 5.0 fusion.393
  738.9 4.8 multiply_convert_fusion.6
  749.2 5.2 multiply_convert_fusion.7
  754.4 5.2 fusion.384
  770.9 119.5 %all-reduce.29.cloned.1.call-done = (bf16[256,2048]{1,0:T(8,128)(2,1)}, bf16[256,2048]{1,0:T(8,128)(2,1)}, bf16[256,2048]{1,0:T(8,128)(2,1)}) async-done(((bf16[256,2048]{1,0:T(8,128)(2,1)}, bf16[256,2048]{1,0:T(8,128)(2,1)}, bf16[256,2048]{1,0:T(8,128)(2,1)}), (bf16[256,2048]{1,0:T(8,128)(2,1)}, bf16[256,2048]{1,0:T(8,128)(2,1)}, bf16[256,2048]{1,0:T(8,128)(2,1)})) %all-reduce.29.cloned.1.call-update) | async-done | bytes 3145744 | tf_op jit(solution)/shard_map/psum | solution.py:137
  890.4 7.6 multiply_reduce_fusion
  910.6 5.1 fusion.3
  925.0 6.6 fusion.9
  932.6 6.7 fusion.11
  942.0 6.6 fusion
  949.6 6.8 fusion.2
  959.0 5.1 fusion.6
  974.4 6.0 fusion.91
  985.2 5.9 fusion.88
  997.1 6.1 fusion.85
  1011.1 6.0 fusion.82
  1026.8 7.6 fusion.398
  1034.4 6.5 fusion.396
  1058.6 15.3 reduce-scatter.20.cloned.1.call-done
  1084.1 7.5 fusion.397
  1091.6 22.0 %reduce-scatter.18.cloned.1.call-done = bf16[256,256]{0,1:T(8,128)(2,1)} async-done(((bf16[2048,256]{0,1:T(8,128)(2,1)}), bf16[256,256]{0,1:T(8,128)(2,1)}) %reduce-scatter.18.cloned.1.call-update) | async-done | bytes 131088 | tf_op jit(solution)/shard_map/reduce_scatter | solution.py:168
  1116.7 35.9 %reduce-scatter.22.cloned.1.call-done = bf16[256,256]{0,1:T(8,128)(2,1)} async-done(((bf16[2048,256]{0,1:T(8,128)(2,1)}), bf16[256,256]{0,1:T(8,128)(2,1)}) %reduce-scatter.22.cloned.1.call-update) | async-done | bytes 131088 | tf_op jit(solution)/shard_map/reduce_scatter | solution.py:168
  1156.5 35.3 %reduce-scatter.26.cloned.1.call-done = bf16[256,256]{0,1:T(8,128)(2,1)} async-done(((bf16[2048,256]{0,1:T(8,128)(2,1)}), bf16[256,256]{0,1:T(8,128)(2,1)}) %reduce-scatter.26.cloned.1.call-update) | async-done | bytes 131088 | tf_op jit(solution)/shard_map/reduce_scatter | solution.py:168
  1195.7 35.7 %reduce-scatter.30.cloned.1.call-done = bf16[256,256]{0,1:T(8,128)(2,1)} async-done(((bf16[2048,256]{0,1:T(8,128)(2,1)}), bf16[256,256]{0,1:T(8,128)(2,1)}) %reduce-scatter.30.cloned.1.call-update) | async-done | bytes 131088 | tf_op jit(solution)/shard_map/reduce_scatter | solution.py:168
  1235.1 18.2 add_convert_fusion.2
  1253.5 8.0 fusion.401
  1261.5 6.5 fusion.399
  1268.0 6.4 fusion.400
  1274.4 17.4 add_convert_fusion.1
  1292.9 7.8 fusion.177
  1300.7 6.5 fusion.185
  1307.2 6.3 fusion.181
  1313.5 17.3 add_convert_fusion
  1331.1 5.9 convolution_convert_fusion.5
  1337.0 5.7 convolution_convert_fusion.4
  1372.4 27.0 %reduce-scatter.36.cloned.1.call-done = bf16[256,256]{1,0:T(8,128)(2,1)} async-done(((bf16[2048,256]{1,0:T(8,128)(2,1)}), bf16[256,256]{1,0:T(8,128)(2,1)}) %reduce-scatter.36.cloned.1.call-update) | async-done | bytes 131088 | tf_op jit(solution)/shard_map/reduce_scatter | solution.py:269
  1401.1 64.1 %reduce-scatter.40.cloned.1.call-done = bf16[256,1536]{1,0:T(8,128)(2,1)} async-done(((bf16[2048,1536]{1,0:T(8,128)(2,1)}), bf16[256,1536]{1,0:T(8,128)(2,1)}) %reduce-scatter.40.cloned.1.call-update) | async-done | bytes 786448 | tf_op jit(solution)/shard_map/reduce_scatter | solution.py:275
  1467.7 62.7 %reduce-scatter.42.cloned.1.call-done = bf16[256,1536]{1,0:T(8,128)(2,1)} async-done(((bf16[2048,1536]{1,0:T(8,128)(2,1)}), bf16[256,1536]{1,0:T(8,128)(2,1)}) %reduce-scatter.42.cloned.1.call-update) | async-done | bytes 786448 | tf_op jit(solution)/shard_map/reduce_scatter | solution.py:278
  1532.9 62.4 %reduce-scatter.44.cloned.1.call-done = bf16[1536,256]{1,0:T(8,128)(2,1)} async-done(((bf16[1536,2048]{1,0:T(8,128)(2,1)}), bf16[1536,256]{1,0:T(8,128)(2,1)}) %reduce-scatter.44.cloned.1.call-update) | async-done | bytes 786448 | tf_op jit(solution)/shard_map/reduce_scatter | solution.py:281
  1597.7 292.1 %all-reduce.27.cloned.1.call-done = (bf16[256,2048]{1,0:T(8,128)(2,1)}, bf16[256,2048]{1,0:T(8,128)(2,1)}, bf16[256,2048]{1,0:T(8,128)(2,1)}, bf16[256,2048]{1,0...) async-done(((bf16[256,2048]{1,0:T(8,128)(2,1)}, bf16[256,2048]{1,0:T(8,128)(2,1)}, ...) | async-done | bytes 8388624 | tf_op jit(solution)/shard_map/psum | solution.py:122
  1889.9 6.5 fusion.111
  1913.2 39.5 %all-reduce.16 = (f32[2048]{0:T(1024)}, f32[2048]{0:T(1024)}, f32[128]{0:T(128)}, f32[128]{0:T(128)}) all-reduce(f32[2048]{0:T(1024)S(1)} %add_add_fusion.17, f32[2048]{0:T(1024)S(1)} %add_add_fusion.16, f32[128]{0:T(128)S(1)} %add_add_fusion.19, f32[128]{0:T(128)S(1)} %add_add_fusion.18), channel_id=1, replica_groups=mesh['wide'=8,'narrow'=4] {'wide','narrow'}, use_global_device_ids=true, to_apply=%region_91.92 | all-reduce | flops 4352 | bytes 34816 | tf_op jit(solution)/shard_map/psum | solution.py:285
  (834 shorter events, 318.8 us)
Async XLA Ops:
  7.2 28.8 %all-gather.16.cloned.1.call-start = ((), (), s32[]{:S(2)}) async-start(), calls=%async_computation.15 | async-start | bytes 1179648 | tf_op jit(solution)/shard_map/all_gather | solution.py:249
  7.9 53.4 %all-gather.20.cloned.1.call-start = ((), (), s32[]{:S(2)}) async-start(), calls=%async_computation.17 | async-start | bytes 1179648 | tf_op jit(solution)/shard_map/all_gather | solution.py:248
  8.7 82.3 %all-gather.24.cloned.1.call-start = ((), (), s32[]{:S(2)}) async-start(), calls=%async_computation.19 | async-start | bytes 2359296 | tf_op jit(solution)/shard_map/all_gather | solution.py:247
  9.4 107.3 %all-gather.38.cloned.1.call-start = ((), (), s32[]{:S(2)}) async-start(), calls=%async_computation.26 | async-start | bytes 1179648 | tf_op jit(solution)/shard_map/all_gather | solution.py:97
  14.1 24.8 %copy-start.229 = (f32[256]{0:T(256)}, f32[256]{0:T(256)S(1)}, u32[]{:S(2)}) copy-start(f32[256]{0:T(256)S(1)} %fusion.118) | copy-start | bytes 3076
  14.1 103.9 %copy-start.194 = (f32[256]{0:T(256)}, f32[256]{0:T(256)S(1)}, u32[]{:S(2)}) copy-start(f32[256]{0:T(256)S(1)} %fusion.321) | copy-start | bytes 3076
  38.7 24.1 %copy-start.94 = (f32[2048]{0:T(1024)S(1)}, f32[2048]{0:T(1024)}, u32[]{:S(2)}) copy-start(f32[2048]{0:T(1024)} %param.24) | copy-start | bytes 24580
  38.7 103.8 %all-gather.40.cloned.1.call-start = ((), (), s32[]{:S(2)}) async-start(), calls=%async_computation.27 | async-start | bytes 1179648 | tf_op jit(solution)/shard_map/all_gather | solution.py:96
  39.5 81.9 %copy-start.56 = (f32[256,128]{0,1:T(8,128)}, f32[256,128]{0,1:T(8,128)S(1)}, u32[]{:S(2)}) copy-start(f32[256,128]{0,1:T(8,128)S(1)} %get-tuple-element.143) | copy-start | bytes 393220
  39.5 81.9 %copy-start.96 = (f32[256,128]{0,1:T(8,128)}, f32[256,128]{0,1:T(8,128)S(1)}, u32[]{:S(2)}) copy-start(f32[256,128]{0,1:T(8,128)S(1)} %get-tuple-element.144) | copy-start | bytes 393220
  66.5 105.9 %all-gather.26.cloned.1.call-start = ((), (), s32[]{:S(2)}) async-start(), calls=%async_computation.20 | async-start | bytes 2359296 | tf_op jit(solution)/shard_map/all_gather | solution.py:250
  67.1 160.7 %all-reduce.25.cloned.1.call-start = ((), (), s32[]{:S(2)}) async-start(), calls=%async_computation.28 | async-start | bytes 2097152 | tf_op jit(solution)/shard_map/psum | solution.py:110
  118.1 28.4 %copy-start.81 = (bf16[2048,2,128]{2,1,0:T(2,128)(2,1)}, bf16[2048,2,128]{2,1,0:T(2,128)(2,1)S(1)}, u32[]{:S(2)}) copy-start(bf16[2048,2,128]{2,1,0:T(2,128)(2,1)S(1)} %reshape.1307) | copy-start | bytes 3145732
  121.2 24.1 %copy-start.221 = (f32[256,4]{0,1:T(4,128)}, f32[256,4]{0,1:T(4,128)S(1)}, u32[]{:S(2)}) copy-start(f32[256,4]{0,1:T(4,128)S(1)} %get-tuple-element.185) | copy-start | bytes 12292
  122.2 23.1 %copy-start.132 = (bf16[256,4,128]{0,2,1:T(8,128)(2,1)}, bf16[256,4,128]{0,2,1:T(8,128)(2,1)S(1)}, u32[]{:S(2)}) copy-start(bf16[256,4,128]{0,2,1:T(8,128)(2,1)S(1)} %fusion.246) | copy-start | bytes 786436
  150.3 25.3 %copy-start.156 = (bf16[2,128,2,256]{3,1,2,0:T(8,128)(2,1)}, bf16[2,128,2,256]{3,1,2,0:T(8,128)(2,1)S(1)}, u32[]{:S(2)}) copy-start(bf16[2,128,2,256]{3,1,2,0:T(8,128)(2,1)S(1)} %fusion.167) | copy-start | bytes 786436
  175.7 55.6 %copy-start.40 = (bf16[2048,256]{1,0:T(8,128)(2,1)S(1)}, bf16[2048,256]{1,0:T(8,128)(2,1)}, u32[]{:S(2)}) copy-start(bf16[2048,256]{1,0:T(8,128)(2,1)} %all-gather.16.cloned.1.call-done) | copy-start | bytes 3145732
  175.7 83.8 %all-gather.42.cloned.1.call-start = ((), (), s32[]{:S(2)}) async-start(), calls=%async_computation.29 | async-start | bytes 1179648 | tf_op jit(solution)/shard_map/all_gather | solution.py:97
  231.3 22.6 %copy-start.212 = (f32[256]{0:T(256)}, f32[256]{0:T(256)S(1)}, u32[]{:S(2)}) copy-start(f32[256]{0:T(256)S(1)} %fusion.323) | copy-start | bytes 3076
  233.7 48.7 %all-gather.18.cloned.1.call-start = ((), (), s32[]{:S(2)}) async-start(), calls=%async_computation.16 | async-start | bytes 1179648 | tf_op jit(solution)/shard_map/all_gather | solution.py:97
  234.0 21.7 %copy-start.197 = (f32[256]{0:T(256)}, f32[256]{0:T(256)S(1)}, u32[]{:S(2)}) copy-start(f32[256]{0:T(256)S(1)} %fusion.317) | copy-start | bytes 3076
  236.4 71.8 %all-gather.34.cloned.1.call-start = ((), (), s32[]{:S(2)}) async-start(), calls=%async_computation.24 | async-start | bytes 1179648 | tf_op jit(solution)/shard_map/all_gather | solution.py:97
  236.9 20.6 %copy-start.58 = (f32[256,128]{0,1:T(8,128)}, f32[256,128]{0,1:T(8,128)S(1)}, u32[]{:S(2)}) copy-start(f32[256,128]{0,1:T(8,128)S(1)} %get-tuple-element.141) | copy-start | bytes 393220
  236.9 20.6 %copy-start.98 = (f32[256,128]{0,1:T(8,128)}, f32[256,128]{0,1:T(8,128)S(1)}, u32[]{:S(2)}) copy-start(f32[256,128]{0,1:T(8,128)S(1)} %get-tuple-element.142) | copy-start | bytes 393220
  237.0 14.0 copy-start.199
  241.7 92.4 %all-gather.44.cloned.1.call-start = ((), (), s32[]{:S(2)}) async-start(), calls=%async_computation.30 | async-start | bytes 1179648 | tf_op jit(solution)/shard_map/all_gather | solution.py:96
  246.5 112.8 %all-gather.22.cloned.1.call-start = ((), (), s32[]{:S(2)}) async-start(), calls=%async_computation.18 | async-start | bytes 1179648 | tf_op jit(solution)/shard_map/all_gather | solution.py:96
  247.1 10.6 copy-start.62
  247.9 136.9 %all-gather.36.cloned.1.call-start = ((), (), s32[]{:S(2)}) async-start(), calls=%async_computation.25 | async-start | bytes 1179648 | tf_op jit(solution)/shard_map/all_gather | solution.py:96
  249.2 182.8 %all-gather.28.cloned.1.call-start = ((), (), s32[]{:S(2)}) async-start(), calls=%async_computation.21 | async-start | bytes 7077888 | tf_op jit(solution)/shard_map/all_gather | solution.py:251
  249.7 230.5 %all-gather.32.cloned.1.call-start = ((), (), s32[]{:S(2)}) async-start(), calls=%async_computation.23 | async-start | bytes 7077888 | tf_op jit(solution)/shard_map/all_gather | solution.py:253
  250.3 277.1 %all-gather.30.cloned.1.call-start = ((), (), s32[]{:S(2)}) async-start(), calls=%async_computation.22 | async-start | bytes 7077888 | tf_op jit(solution)/shard_map/all_gather | solution.py:252
  250.9 447.3 %all-reduce.31.cloned.1.call-start = ((), (), s32[]{:S(2)}) async-start(), calls=%async_computation.48 | async-start | bytes 8388608 | tf_op jit(solution)/shard_map/psum | solution.py:110
  257.7 76.5 %copy-start.136 = (bf16[256,4,128]{0,2,1:T(8,128)(2,1)}, bf16[256,4,128]{0,2,1:T(8,128)(2,1)S(1)}, u32[]{:S(2)}) copy-start(bf16[256,4,128]{0,2,1:T(8,128)(2,1)S(1)} %fusion.248) | copy-start | bytes 786436
  259.0 125.8 %copy-start.134 = (bf16[256,4,128]{0,2,1:T(8,128)(2,1)}, bf16[256,4,128]{0,2,1:T(8,128)(2,1)S(1)}, u32[]{:S(2)}) copy-start(bf16[256,4,128]{0,2,1:T(8,128)(2,1)S(1)} %fusion.244) | copy-start | bytes 786436
  259.5 267.9 %copy-start.50 = (bf16[256,2048]{1,0:T(8,128)(2,1)}, bf16[256,2048]{1,0:T(8,128)(2,1)S(1)}, u32[]{:S(2)}) copy-start(bf16[256,2048]{1,0:T(8,128)(2,1)S(1)} %multiply_convert_fusion.1) | copy-start | bytes 3145732
  543.0 347.4 %all-reduce.29.cloned.1.call-start = ((), (), s32[]{:S(2)}) async-start(), calls=%async_computation.47 | async-start | bytes 6291456 | tf_op jit(solution)/shard_map/psum | solution.py:137
  706.5 12.8 copy-start.45
  706.5 18.7 copy-start.47
  733.0 26.6 %copy-start.110 = (bf16[256,1536]{1,0:T(8,128)(2,1)}, bf16[256,1536]{1,0:T(8,128)(2,1)S(1)}, u32[]{:S(2)}) copy-start(bf16[256,1536]{1,0:T(8,128)(2,1)S(1)} %get-tuple-element.99) | copy-start | bytes 2359300
  743.7 19.4 copy-start.106
  754.4 12.2 copy-start.108
  770.1 278.1 %reduce-scatter.24.cloned.1.call-start = ((), (), s32[]{:S(2)}) async-start(), calls=%async_computation.35 | async-start | bytes 1179648 | tf_op jit(solution)/shard_map/reduce_scatter | solution.py:162
  770.8 144.9 %copy-start.190 = (f32[2,2,256]{2,1,0:T(2,128)}, f32[2,2,256]{2,1,0:T(2,128)S(1)}, u32[]{:S(2)}) copy-start(f32[2,2,256]{2,1,0:T(2,128)S(1)} %log_add_fusion.1) | copy-start | bytes 12292
  770.8 178.7 %copy-start.188 = (f32[2,2,256]{2,1,0:T(2,128)}, f32[2,2,256]{2,1,0:T(2,128)S(1)}, u32[]{:S(2)}) copy-start(f32[2,2,256]{2,1,0:T(2,128)S(1)} %log_add_fusion) | copy-start | bytes 12292
  920.7 129.1 %reduce-scatter.16.cloned.1.call-start = ((), (), s32[]{:S(2)}) async-start(), calls=%async_computation.31 | async-start | bytes 1179648 | tf_op jit(solution)/shard_map/reduce_scatter | solution.py:162
  941.9 109.7 %reduce-scatter.28.cloned.1.call-start = ((), (), s32[]{:S(2)}) async-start(), calls=%async_computation.37 | async-start | bytes 1179648 | tf_op jit(solution)/shard_map/reduce_scatter | solution.py:162
  958.9 114.9 %reduce-scatter.20.cloned.1.call-start = ((), (), s32[]{:S(2)}) async-start(), calls=%async_computation.33 | async-start | bytes 1179648 | tf_op jit(solution)/shard_map/reduce_scatter | solution.py:162
  969.1 144.5 %reduce-scatter.18.cloned.1.call-start = ((), (), s32[]{:S(2)}) async-start(), calls=%async_computation.32 | async-start | bytes 1179648 | tf_op jit(solution)/shard_map/reduce_scatter | solution.py:168
  980.4 172.2 %reduce-scatter.22.cloned.1.call-start = ((), (), s32[]{:S(2)}) async-start(), calls=%async_computation.34 | async-start | bytes 1179648 | tf_op jit(solution)/shard_map/reduce_scatter | solution.py:168
  991.2 200.6 %reduce-scatter.26.cloned.1.call-start = ((), (), s32[]{:S(2)}) async-start(), calls=%async_computation.36 | async-start | bytes 1179648 | tf_op jit(solution)/shard_map/reduce_scatter | solution.py:168
  1003.1 228.3 %reduce-scatter.30.cloned.1.call-start = ((), (), s32[]{:S(2)}) async-start(), calls=%async_computation.38 | async-start | bytes 1179648 | tf_op jit(solution)/shard_map/reduce_scatter | solution.py:168
  1017.1 349.9 %reduce-scatter.32.cloned.1.call-start = ((), (), s32[]{:S(2)}) async-start(), calls=%async_computation.39 | async-start | bytes 2359296 | tf_op jit(solution)/shard_map/reduce_scatter | solution.py:263
  1025.6 343.1 %reduce-scatter.38.cloned.1.call-start = ((), (), s32[]{:S(2)}) async-start(), calls=%async_computation.42 | async-start | bytes 2359296 | tf_op jit(solution)/shard_map/reduce_scatter | solution.py:272
  1048.1 322.7 %reduce-scatter.34.cloned.1.call-start = ((), (), s32[]{:S(2)}) async-start(), calls=%async_computation.40 | async-start | bytes 1179648 | tf_op jit(solution)/shard_map/reduce_scatter | solution.py:266
  1052.6 22.2 %copy-start.128 = (f32[256,2,128]{0,2,1:T(8,128)S(1)}, f32[256,2,128]{0,2,1:T(8,128)}, u32[]{:S(2)}) copy-start(f32[256,2,128]{0,2,1:T(8,128)} %copy-done.127) | copy-start | bytes 786436
  1055.5 22.9 %copy-start.131 = (f32[256,2,128]{0,2,1:T(8,128)S(1)}, f32[256,2,128]{0,2,1:T(8,128)}, u32[]{:S(2)}) copy-start(f32[256,2,128]{0,2,1:T(8,128)} %copy-done.130) | copy-start | bytes 786436
  1083.6 315.9 %reduce-scatter.36.cloned.1.call-start = ((), (), s32[]{:S(2)}) async-start(), calls=%async_computation.41 | async-start | bytes 1179648 | tf_op jit(solution)/shard_map/reduce_scatter | solution.py:269
  1235.0 230.2 %reduce-scatter.40.cloned.1.call-start = ((), (), s32[]{:S(2)}) async-start(), calls=%async_computation.43 | async-start | bytes 7077888 | tf_op jit(solution)/shard_map/reduce_scatter | solution.py:275
  1253.3 277.1 %reduce-scatter.42.cloned.1.call-start = ((), (), s32[]{:S(2)}) async-start(), calls=%async_computation.44 | async-start | bytes 7077888 | tf_op jit(solution)/shard_map/reduce_scatter | solution.py:278
  1291.8 303.5 %reduce-scatter.44.cloned.1.call-start = ((), (), s32[]{:S(2)}) async-start(), calls=%async_computation.45 | async-start | bytes 7077888 | tf_op jit(solution)/shard_map/reduce_scatter | solution.py:281
  1330.8 559.0 %all-reduce.27.cloned.1.call-start = ((), (), s32[]{:S(2)}) async-start(), calls=%async_computation.46 | async-start | bytes 16777216 | tf_op jit(solution)/shard_map/psum | solution.py:122
  1331.1 11.6 slice-start.8
  1467.7 422.1 %copy-start.202 = (f32[256]{0:T(256)S(1)}, f32[256]{0:T(256)}, u32[]{:S(2)}) copy-start(f32[256]{0:T(256)} %copy-done.199) | copy-start | bytes 3076
  (235 other events, 875.2 us)
Sparse Core Ops, SparseCore 0:
  9.9 26.0 all-gather.15
  37.9 23.3 all-gather.19
  63.2 27.7 all-gather.23
  93.3 23.3 all-gather.37
  119.0 23.4 all-gather.39
  144.3 28.0 all-gather.25
  175.8 51.8 all-reduce.24
  233.9 22.6 all-gather.41
  259.0 23.3 all-gather.17
  284.8 23.3 all-gather.33
  310.6 23.4 all-gather.43
  335.9 23.4 all-gather.21
  361.2 23.4 all-gather.35
  386.5 45.3 all-gather.27
  433.6 46.5 all-gather.31
  482.0 45.3 all-gather.29
  543.1 155.0 all-reduce.30
  770.3 120.0 all-reduce.28
  920.9 34.9 reduce-scatter.23
  959.5 35.9 reduce-scatter.15
  998.7 35.9 reduce-scatter.27
  1037.8 35.9 reduce-scatter.19
  1077.6 35.9 reduce-scatter.17
  1116.6 35.9 reduce-scatter.21
  1155.8 35.9 reduce-scatter.25
  1195.4 35.9 reduce-scatter.29
  1234.5 41.1 reduce-scatter.31
  1279.0 41.1 reduce-scatter.37
  1323.9 35.9 reduce-scatter.33
  1363.5 35.9 reduce-scatter.35
  1403.4 61.7 reduce-scatter.39
  1468.6 61.7 reduce-scatter.41
  1533.7 61.5 reduce-scatter.43
  1598.7 291.0 all-reduce.26
where the time goes:
time: 1970 us; the launch traced here: 1960 us
  waiting for transfers between devices  1330 us (68%)
  matrix products  388 us (20%)
  other arithmetic  128 us (6%)
  local copies, waits for them, and re-layouts  54.3 us (3%)
  blocking collectives  39.5 us (2%)
    psum x1, waiting for transfers between devices, one_batch(): lax.psum(ffn_part.astype(jnp.bfloat16), 'narrow').astype(jnp.float32)  292 us
    psum x2, waiting for transfers between devices, one_batch(): lax.psum(attn_part.astype(jnp.bfloat16), 'narrow').astype(jnp.float32)  207 us
    reduce_scatter x4, waiting for transfers between devices, one_batch(): lax.psum_scatter(grad_valueall.reshape(total, groups * HD).astype(jnp.bfl...  129 us
    psum x1, waiting for transfers between devices, one_batch(): lax.psum(partial_two.astype(jnp.bfloat16), 'narrow').astype(jnp.float32)  119 us
    all_gather x4, waiting for transfers between devices, one_batch(): lax.all_gather(key_low, 'wide', axis=0, tiled=True)  74 us
    all_gather x4, waiting for transfers between devices, one_batch(): lax.all_gather(value_low, 'wide', axis=0, tiled=True)  65.8 us
    reduce_scatter x1, waiting for transfers between devices, local(): lax.psum_scatter(totals[4].astype(jnp.bfloat16), 'wide', scatter_dimensio...  64.1 us
    reduce_scatter x1, waiting for transfers between devices, local(): lax.psum_scatter(totals[5].astype(jnp.bfloat16), 'wide', scatter_dimensio...  62.7 us
  transfers between devices with their start and end apart: 34, of which 28 were waited for; matrix products, arithmetic and copies ran while one was open for 20% of the time, Pallas kernels for 0%

commit v1 on v0

--- a/solution.py
+++ b/solution.py
@@ -8,6 +8,28 @@
 NDOC = 8
 EPSILON = 1e-06
 THETA = 1000000.0
+
+
+def laid_out(pieces, dim):
+    lengths = list(pieces.shape[1:])
+    lengths[dim] *= pieces.shape[0]
+    return jnp.moveaxis(pieces, 0, dim).reshape(lengths)
+
+
+def collect(x, axis, dim):
+    size = lax.axis_size(axis)
+    pairs = [(i, (i + 1) % size) for i in range(size)]
+    back = [(b, a) for a, b in pairs]
+    lower, upper = ([], [])
+    for step in range(size - 1):
+        if step % 2 == 0:
+            lower.append(lax.ppermute(lower[-1] if lower else x, axis, pairs))
+        else:
+            upper.append(lax.ppermute(upper[-1] if upper else x, axis, back))
+    blocks = jnp.stack([*lower[::-1], x, *upper])
+    shift = lax.axis_index(axis) - len(lower)
+    blocks = blocks[(jnp.arange(size) - shift) % size]
+    return laid_out(blocks, dim)
 
 
 def rms_norm(values, gain):
@@ -94,7 +116,7 @@
     key_low = key_turned.astype(jnp.bfloat16).reshape(tok_rows, groups * HD)
     key_all, value_all = (
         lax.all_gather(key_low, "wide", axis=0, tiled=True),
-        lax.all_gather(value_low, "wide", axis=0, tiled=True),
+        collect(value_low, "wide", 0),
     )
     key_all = key_all.reshape(total, groups, HD)
     value_all = value_all.reshape(total, groups, HD)

time: 1970 us -> 1880 us (0.954)
  waiting for transfers between devices: 1330 us -> 1200 us
  starting transfers between devices: 3.13 us -> 29.5 us
    all_gather x4 -> x0, waiting for transfers between devices: 65.8 us -> none  [one_batch(): lax.all_gather(value_low, 'wide', axis=0, tiled=True)]
    all_gather x4, waiting for transfers between devices: 74 us -> 17.8 us  [one_batch(): lax.all_gather(key_low, 'wide', axis=0, tiled=True)]
    ppermute x0 -> x28, waiting for transfers between devices: none -> 26.9 us  [the longest x16 21 us: collect(): lower.append(lax.ppermute(lower[-1] if lower else x, axis, pairs))]
    ppermute x0 -> x28, starting transfers between devices: none -> 26.6 us  [the longest x12 25.8 us: collect(): upper.append(lax.ppermute(upper[-1] if upper else x, axis, back))]
    unnamed x530 -> x586, local copies, waits for them, and re-layouts: 37 us -> 51.2 us
  transfers between devices with their start and end apart: 34 -> 58, of which waited for: 28 -> 33; matrix products, arithmetic and copies ran while one was open for 20% -> 21% of each run, Pallas kernels for 0% -> 0%
where the time goes in v1:
time: 1880 us; the launch traced here: 1870 us
  waiting for transfers between devices  1200 us (64%)
  matrix products  377 us (20%)
  other arithmetic  132 us (7%)
  local copies, waits for them, and re-layouts  72.7 us (4%)
  blocking collectives  39.5 us (2%)
  starting transfers between devices  29.5 us (2%)
    psum x1, waiting for transfers between devices, one_batch(): lax.psum(ffn_part.astype(jnp.bfloat16), 'narrow').astype(jnp.float32)  292 us
    psum x2, waiting for transfers between devices, one_batch(): lax.psum(attn_part.astype(jnp.bfloat16), 'narrow').astype(jnp.float32)  206 us
    reduce_scatter x4, waiting for transfers between devices, one_batch(): lax.psum_scatter(grad_valueall.reshape(total, groups * HD).astype(jnp.bfl...  129 us
    psum x1, waiting for transfers between devices, one_batch(): lax.psum(partial_two.astype(jnp.bfloat16), 'narrow').astype(jnp.float32)  119 us
    reduce_scatter x1, waiting for transfers between devices, local(): lax.psum_scatter(totals[4].astype(jnp.bfloat16), 'wide', scatter_dimensio...  64 us
    reduce_scatter x1, waiting for transfers between devices, local(): lax.psum_scatter(totals[5].astype(jnp.bfloat16), 'wide', scatter_dimensio...  62.7 us
    reduce_scatter x1, waiting for transfers between devices, local(): lax.psum_scatter(totals[6].astype(jnp.bfloat16), 'wide', scatter_dimensio...  62.6 us
    unnamed x586, local copies, waits for them, and re-layouts  51.2 us
  transfers between devices with their start and end apart: 58, of which 33 were waited for; matrix products, arithmetic and copies ran while one was open for 21% of the time, Pallas kernels for 0%

profile of v1, /device:TPU:0, one launch (start us, length us, event | category | flops | bytes accessed | tf_op | source)
XLA Modules:
  0.0 1867.6 jit_solution(13487367570994140306)
XLA Ops:
  15.6 20.4 %all-gather.14.cloned.1.call-done = bf16[2048,256]{1,0:T(8,128)(2,1)} async-done(((bf16[256,256]{1,0:T(8,128)(2,1)}), bf16[2048,256]{1,0:T(8,128)(2,1)}) %all-gather.14.cloned.1.call-update) | async-done | bytes 1048592 | tf_op jit(solution)/shard_map/all_gather | solution.py:270
  41.9 19.5 %all-gather.12.cloned.1.call-done = bf16[2048,256]{1,0:T(8,128)(2,1)} async-done(((bf16[256,256]{1,0:T(8,128)(2,1)}), bf16[2048,256]{1,0:T(8,128)(2,1)}) %all-gather.12.cloned.1.call-update) | async-done | bytes 1048592 | tf_op jit(solution)/shard_map/all_gather | solution.py:271
  63.7 5.1 collective-permute-done.14
  71.7 4.4 collective-permute-done.15
  76.0 4.6 fusion.147
  83.9 4.6 collective-permute-done.19
  103.4 17.7 all-gather.30.cloned.1.call-done
  128.9 22.1 %all-gather.20.cloned.1.call-done = bf16[512,2048]{1,0:T(8,128)(2,1)} async-done(((bf16[512,256]{1,0:T(8,128)(2,1)}), bf16[512,2048]{1,0:T(8,128)(2,1)}) %all-gather.20.cloned.1.call-update) | async-done | bytes 2097168 | tf_op jit(solution)/shard_map/all_gather | solution.py:272
  155.1 51.3 %all-reduce.25.cloned.1.call-done = bf16[256,2048]{1,0:T(8,128)(2,1)} async-done(((bf16[256,2048]{1,0:T(8,128)(2,1)}), bf16[256,2048]{1,0:T(8,128)(2,1)}) %all-reduce.25.cloned.1.call-update) | async-done | bytes 1048592 | tf_op jit(solution)/shard_map/psum | solution.py:132
  314.6 25.1 %all-gather.22.cloned.1.call-done = bf16[2048,1536]{1,0:T(8,128)(2,1)} async-done(((bf16[256,1536]{1,0:T(8,128)(2,1)}), bf16[2048,1536]{1,0:T(8,128)(2,1)}) %all-gather.22.cloned.1.call-update) | async-done | bytes 6291472 | tf_op jit(solution)/shard_map/all_gather | solution.py:273
  339.7 5.7 fusion.383
  345.4 42.8 %all-gather.26.cloned.1.call-done = bf16[1536,2048]{1,0:T(8,128)(2,1)} async-done(((bf16[1536,256]{1,0:T(8,128)(2,1)}), bf16[1536,2048]{1,0:T(8,128)(2,1)}) %all-gather.26.cloned.1.call-update) | async-done | bytes 6291472 | tf_op jit(solution)/shard_map/all_gather | solution.py:275
  388.2 6.1 fusion.179
  394.2 41.1 %all-gather.24.cloned.1.call-done = bf16[2048,1536]{1,0:T(8,128)(2,1)} async-done(((bf16[256,1536]{1,0:T(8,128)(2,1)}), bf16[2048,1536]{1,0:T(8,128)(2,1)}) %all-gather.24.cloned.1.call-update) | async-done | bytes 6291472 | tf_op jit(solution)/shard_map/all_gather | solution.py:274
  435.3 6.8 multiply_convert_fusion.9
  442.1 5.2 fusion.392
  451.0 155.1 %all-reduce.31.cloned.1.call-done = (bf16[256,2048]{1,0:T(8,128)(2,1)}, bf16[256,2048]{1,0:T(8,128)(2,1)}, bf16[256,2048]{1,0:T(8,128)(2,1)}, bf16[256,2048]{1,0:T(8,128)(2,1)}) async-done(((bf16[256,2048]{1,0:T(8,128)(2,1)}, bf16[256,2048]{1,0:T(8,128)(2,1)}, bf16[256,2048]{1,0:T(8,128)(2,1)}, bf16[256,2048]{1,0:T(8,128)(2,1)}), (bf16[256,2048]{1,0:T(8,128)(2,1)}, bf16[256,2048]{1,0:T(8,128)(2,1)}, ...) | async-done | bytes 4194320 | tf_op jit(solution)/shard_map/psum | solution.py:132
  606.1 6.1 multiply_reduce_fusion.1
  614.5 6.9 fusion.384
  641.8 5.0 fusion.395
  646.7 4.8 multiply_convert_fusion.6
  652.5 4.6 fusion.389
  657.1 5.2 multiply_convert_fusion.7
  662.3 5.2 fusion.386
  678.9 119.4 %all-reduce.29.cloned.1.call-done = (bf16[256,2048]{1,0:T(8,128)(2,1)}, bf16[256,2048]{1,0:T(8,128)(2,1)}, bf16[256,2048]{1,0:T(8,128)(2,1)}) async-done(((bf16[256,2048]{1,0:T(8,128)(2,1)}, bf16[256,2048]{1,0:T(8,128)(2,1)}, bf16[256,2048]{1,0:T(8,128)(2,1)}), (bf16[256,2048]{1,0:T(8,128)(2,1)}, bf16[256,2048]{1,0:T(8,128)(2,1)}, bf16[256,2048]{1,0:T(8,128)(2,1)})) %all-reduce.29.cloned.1.call-update) | async-done | bytes 3145744 | tf_op jit(solution)/shard_map/psum | solution.py:159
  798.3 7.6 multiply_reduce_fusion
  809.8 4.7 fusion.129
  818.5 5.0 fusion.3
  832.9 6.6 fusion.9
  840.5 6.7 fusion.11
  849.8 6.5 fusion
  857.4 6.8 fusion.2
  866.8 5.0 fusion.6
  882.3 5.9 fusion.91
  893.0 6.0 fusion.88
  904.9 6.0 fusion.85
  918.9 6.0 fusion.82
  934.7 7.6 fusion.400
  942.3 6.5 fusion.398
  966.4 15.1 reduce-scatter.20.cloned.1.call-done
  991.7 7.5 fusion.399
  999.2 22.1 %reduce-scatter.18.cloned.1.call-done = bf16[256,256]{0,1:T(8,128)(2,1)} async-done(((bf16[2048,256]{0,1:T(8,128)(2,1)}), bf16[256,256]{0,1:T(8,128)(2,1)}) %reduce-scatter.18.cloned.1.call-update) | async-done | bytes 131088 | tf_op jit(solution)/shard_map/reduce_scatter | solution.py:190
  1024.4 35.9 %reduce-scatter.22.cloned.1.call-done = bf16[256,256]{0,1:T(8,128)(2,1)} async-done(((bf16[2048,256]{0,1:T(8,128)(2,1)}), bf16[256,256]{0,1:T(8,128)(2,1)}) %reduce-scatter.22.cloned.1.call-update) | async-done | bytes 131088 | tf_op jit(solution)/shard_map/reduce_scatter | solution.py:190
  1064.2 35.3 %reduce-scatter.26.cloned.1.call-done = bf16[256,256]{0,1:T(8,128)(2,1)} async-done(((bf16[2048,256]{0,1:T(8,128)(2,1)}), bf16[256,256]{0,1:T(8,128)(2,1)}) %reduce-scatter.26.cloned.1.call-update) | async-done | bytes 131088 | tf_op jit(solution)/shard_map/reduce_scatter | solution.py:190
  1103.3 35.8 %reduce-scatter.30.cloned.1.call-done = bf16[256,256]{0,1:T(8,128)(2,1)} async-done(((bf16[2048,256]{0,1:T(8,128)(2,1)}), bf16[256,256]{0,1:T(8,128)(2,1)}) %reduce-scatter.30.cloned.1.call-update) | async-done | bytes 131088 | tf_op jit(solution)/shard_map/reduce_scatter | solution.py:190
  1142.8 18.2 add_convert_fusion.2
  1161.3 8.0 fusion.403
  1169.2 6.5 fusion.401
  1175.7 6.3 fusion.402
  1182.1 17.4 add_convert_fusion.1
  1200.6 7.8 fusion.177
  1208.4 6.5 fusion.185
  1214.8 6.3 fusion.181
  1221.1 17.3 add_convert_fusion
  1238.8 5.9 convolution_convert_fusion.5
  1244.7 5.7 convolution_convert_fusion.4
  1280.1 27.2 %reduce-scatter.36.cloned.1.call-done = bf16[256,256]{1,0:T(8,128)(2,1)} async-done(((bf16[2048,256]{1,0:T(8,128)(2,1)}), bf16[256,256]{1,0:T(8,128)(2,1)}) %reduce-scatter.36.cloned.1.call-update) | async-done | bytes 131088 | tf_op jit(solution)/shard_map/reduce_scatter | solution.py:291
  1308.9 64.0 %reduce-scatter.40.cloned.1.call-done = bf16[256,1536]{1,0:T(8,128)(2,1)} async-done(((bf16[2048,1536]{1,0:T(8,128)(2,1)}), bf16[256,1536]{1,0:T(8,128)(2,1)}) %reduce-scatter.40.cloned.1.call-update) | async-done | bytes 786448 | tf_op jit(solution)/shard_map/reduce_scatter | solution.py:297
  1375.4 62.7 %reduce-scatter.42.cloned.1.call-done = bf16[256,1536]{1,0:T(8,128)(2,1)} async-done(((bf16[2048,1536]{1,0:T(8,128)(2,1)}), bf16[256,1536]{1,0:T(8,128)(2,1)}) %reduce-scatter.42.cloned.1.call-update) | async-done | bytes 786448 | tf_op jit(solution)/shard_map/reduce_scatter | solution.py:300
  1440.5 62.6 %reduce-scatter.44.cloned.1.call-done = bf16[1536,256]{1,0:T(8,128)(2,1)} async-done(((bf16[1536,2048]{1,0:T(8,128)(2,1)}), bf16[1536,256]{1,0:T(8,128)(2,1)}) %reduce-scatter.44.cloned.1.call-update) | async-done | bytes 786448 | tf_op jit(solution)/shard_map/reduce_scatter | solution.py:303
  1505.5 291.9 %all-reduce.27.cloned.1.call-done = (bf16[256,2048]{1,0:T(8,128)(2,1)}, bf16[256,2048]{1,0:T(8,128)(2,1)}, bf16[256,2048]{1,0:T(8,128)(2,1)}, bf16[256,2048]{1,0...) async-done(((bf16[256,2048]{1,0:T(8,128)(2,1)}, bf16[256,2048]{1,0:T(8,128)(2,1)}, ...) | async-done | bytes 8388624 | tf_op jit(solution)/shard_map/psum | solution.py:144
  1797.5 6.5 fusion.111
  1810.6 4.2 fusion.103
  1820.8 39.5 %all-reduce.16 = (f32[2048]{0:T(1024)}, f32[2048]{0:T(1024)}, f32[128]{0:T(128)}, f32[128]{0:T(128)}) all-reduce(f32[2048]{0:T(1024)S(1)} %add_add_fusion.17, f32[2048]{0:T(1024)S(1)} %add_add_fusion.16, f32[128]{0:T(128)S(1)} %add_add_fusion.19, f32[128]{0:T(128)S(1)} %add_add_fusion.18), channel_id=1, replica_groups=mesh['wide'=8,'narrow'=4] {'wide','narrow'}, use_global_device_ids=true, to_apply=%region_91.92 | all-reduce | flops 4352 | bytes 34816 | tf_op jit(solution)/shard_map/psum | solution.py:307
  (944 shorter events, 351.3 us)
Async XLA Ops:
  7.2 28.9 %all-gather.14.cloned.1.call-start = ((), (), s32[]{:S(2)}) async-start(), calls=%async_computation.16 | async-start | bytes 1179648 | tf_op jit(solution)/shard_map/all_gather | solution.py:270
  7.9 53.4 %all-gather.12.cloned.1.call-start = ((), (), s32[]{:S(2)}) async-start(), calls=%async_computation.15 | async-start | bytes 1179648 | tf_op jit(solution)/shard_map/all_gather | solution.py:271
  8.7 86.6 %all-gather.18.cloned.1.call-start = ((), (), s32[]{:S(2)}) async-start(), calls=%async_computation.18 | async-start | bytes 2359296 | tf_op jit(solution)/shard_map/all_gather | solution.py:269
  9.4 111.7 %all-gather.30.cloned.1.call-start = ((), (), s32[]{:S(2)}) async-start(), calls=%async_computation.24 | async-start | bytes 1179648 | tf_op jit(solution)/shard_map/all_gather | solution.py:118
  14.0 88.8 %copy-start.57 = (f32[256,128]{0,1:T(8,128)}, f32[256,128]{0,1:T(8,128)S(1)}, u32[]{:S(2)}) copy-start(f32[256,128]{0,1:T(8,128)S(1)} %get-tuple-element.143) | copy-start | bytes 393220
  41.2 109.7 %all-gather.20.cloned.1.call-start = ((), (), s32[]{:S(2)}) async-start(), calls=%async_computation.19 | async-start | bytes 2359296 | tf_op jit(solution)/shard_map/all_gather | solution.py:272
  41.8 164.6 %all-reduce.25.cloned.1.call-start = ((), (), s32[]{:S(2)}) async-start(), calls=%async_computation.25 | async-start | bytes 2097152 | tf_op jit(solution)/shard_map/psum | solution.py:132
  63.4 5.3 collective-permute-start.14
  68.7 7.3 collective-permute-start.15
  69.0 11.6 collective-permute-start.18
  76.0 7.3 collective-permute-start.16
  80.6 7.9 collective-permute-start.19
  83.3 9.2 collective-permute-start.17
  88.5 5.4 collective-permute-start.20
  154.3 129.6 %all-gather.32.cloned.1.call-start = ((), (), s32[]{:S(2)}) async-start(), calls=%async_computation.26 | async-start | bytes 1179648 | tf_op jit(solution)/shard_map/all_gather | solution.py:118
  214.5 79.7 %all-gather.16.cloned.1.call-start = ((), (), s32[]{:S(2)}) async-start(), calls=%async_computation.17 | async-start | bytes 1179648 | tf_op jit(solution)/shard_map/all_gather | solution.py:118
  215.8 88.6 %all-gather.28.cloned.1.call-start = ((), (), s32[]{:S(2)}) async-start(), calls=%async_computation.23 | async-start | bytes 1179648 | tf_op jit(solution)/shard_map/all_gather | solution.py:118
  217.1 122.6 %all-gather.22.cloned.1.call-start = ((), (), s32[]{:S(2)}) async-start(), calls=%async_computation.20 | async-start | bytes 7077888 | tf_op jit(solution)/shard_map/all_gather | solution.py:273
  217.7 170.5 %all-gather.26.cloned.1.call-start = ((), (), s32[]{:S(2)}) async-start(), calls=%async_computation.22 | async-start | bytes 7077888 | tf_op jit(solution)/shard_map/all_gather | solution.py:275
  218.4 216.9 %all-gather.24.cloned.1.call-start = ((), (), s32[]{:S(2)}) async-start(), calls=%async_computation.21 | async-start | bytes 7077888 | tf_op jit(solution)/shard_map/all_gather | solution.py:274
  219.0 387.1 %all-reduce.31.cloned.1.call-start = ((), (), s32[]{:S(2)}) async-start(), calls=%async_computation.44 | async-start | bytes 8388608 | tf_op jit(solution)/shard_map/psum | solution.py:132
  225.8 8.7 collective-permute-start.21
  225.9 9.6 collective-permute-start.25
  229.0 9.1 collective-permute-start
  229.0 9.5 collective-permute-start.4
  233.0 7.0 collective-permute-start.7
  234.4 200.9 %copy-start.51 = (bf16[256,2048]{1,0:T(8,128)(2,1)}, bf16[256,2048]{1,0:T(8,128)(2,1)S(1)}, u32[]{:S(2)}) copy-start(bf16[256,2048]{1,0:T(8,128)(2,1)S(1)} %multiply_convert_fusion.1) | copy-start | bytes 3145732
  234.5 8.2 collective-permute-start.22
  235.5 7.3 collective-permute-start.11
  238.1 7.4 collective-permute-start.26
  238.5 9.1 collective-permute-start.1
  239.9 7.7 collective-permute-start.8
  242.8 7.6 collective-permute-start.23
  242.8 8.4 collective-permute-start.5
  245.5 8.3 collective-permute-start.12
  247.6 8.2 collective-permute-start.2
  247.6 9.0 collective-permute-start.9
  250.4 9.0 collective-permute-start.24
  251.2 13.1 collective-permute-start.27
  253.8 15.8 collective-permute-start.6
  255.8 24.1 %collective-permute-start.13 = (bf16[256,256]{1,0:T(8,128)(2,1)S(1)}, bf16[256,256]{1,0:T(8,128)(2,1)S(1)}, u32[]{:S(2)}, u32[]{:S(2)}) collective-permute-start(bf16[256,256]{1,0:T(8,128)(2,1)S(1)} %collective-permute-done.12), channel_id=1, source_target_pairs={{4,0},{8,4},{12,8},{16,12},{20,16},{24,20},{28,24},{0,28},{5,1},{9... | collective-permute-start | bytes 393224 | tf_op jit(solution)/shard_map/ppermute | solution.py:28
  256.7 6.1 collective-permute-start.3
  259.4 14.1 collective-permute-start.10
  450.9 155.2 %copy-start.232 = (f32[256]{0:T(256)S(1)}, f32[256]{0:T(256)}, u32[]{:S(2)}) copy-start(f32[256]{0:T(256)} %copy-done.231) | copy-start | bytes 3076
  450.9 347.4 %all-reduce.29.cloned.1.call-start = ((), (), s32[]{:S(2)}) async-start(), calls=%async_computation.43 | async-start | bytes 6291456 | tf_op jit(solution)/shard_map/psum | solution.py:159
  678.1 277.9 %reduce-scatter.24.cloned.1.call-start = ((), (), s32[]{:S(2)}) async-start(), calls=%async_computation.31 | async-start | bytes 1179648 | tf_op jit(solution)/shard_map/reduce_scatter | solution.py:184
  678.8 144.7 %copy-start.197 = (f32[2,2,256]{2,1,0:T(2,128)}, f32[2,2,256]{2,1,0:T(2,128)S(1)}, u32[]{:S(2)}) copy-start(f32[2,2,256]{2,1,0:T(2,128)S(1)} %log_add_fusion.1) | copy-start | bytes 12292
  678.8 178.6 %copy-start.195 = (f32[2,2,256]{2,1,0:T(2,128)}, f32[2,2,256]{2,1,0:T(2,128)S(1)}, u32[]{:S(2)}) copy-start(f32[2,2,256]{2,1,0:T(2,128)S(1)} %log_add_fusion) | copy-start | bytes 12292
  828.6 129.1 %reduce-scatter.16.cloned.1.call-start = ((), (), s32[]{:S(2)}) async-start(), calls=%async_computation.27 | async-start | bytes 1179648 | tf_op jit(solution)/shard_map/reduce_scatter | solution.py:184
  849.8 109.7 %reduce-scatter.28.cloned.1.call-start = ((), (), s32[]{:S(2)}) async-start(), calls=%async_computation.33 | async-start | bytes 1179648 | tf_op jit(solution)/shard_map/reduce_scatter | solution.py:184
  866.8 114.7 %reduce-scatter.20.cloned.1.call-start = ((), (), s32[]{:S(2)}) async-start(), calls=%async_computation.29 | async-start | bytes 1179648 | tf_op jit(solution)/shard_map/reduce_scatter | solution.py:184
  876.9 144.3 %reduce-scatter.18.cloned.1.call-start = ((), (), s32[]{:S(2)}) async-start(), calls=%async_computation.28 | async-start | bytes 1179648 | tf_op jit(solution)/shard_map/reduce_scatter | solution.py:190
  888.2 172.0 %reduce-scatter.22.cloned.1.call-start = ((), (), s32[]{:S(2)}) async-start(), calls=%async_computation.30 | async-start | bytes 1179648 | tf_op jit(solution)/shard_map/reduce_scatter | solution.py:190
  899.0 200.4 %reduce-scatter.26.cloned.1.call-start = ((), (), s32[]{:S(2)}) async-start(), calls=%async_computation.32 | async-start | bytes 1179648 | tf_op jit(solution)/shard_map/reduce_scatter | solution.py:190
  911.0 228.2 %reduce-scatter.30.cloned.1.call-start = ((), (), s32[]{:S(2)}) async-start(), calls=%async_computation.34 | async-start | bytes 1179648 | tf_op jit(solution)/shard_map/reduce_scatter | solution.py:190
  925.0 349.7 %reduce-scatter.32.cloned.1.call-start = ((), (), s32[]{:S(2)}) async-start(), calls=%async_computation.35 | async-start | bytes 2359296 | tf_op jit(solution)/shard_map/reduce_scatter | solution.py:285
  933.5 342.9 %reduce-scatter.38.cloned.1.call-start = ((), (), s32[]{:S(2)}) async-start(), calls=%async_computation.38 | async-start | bytes 2359296 | tf_op jit(solution)/shard_map/reduce_scatter | solution.py:294
  956.0 322.5 %reduce-scatter.34.cloned.1.call-start = ((), (), s32[]{:S(2)}) async-start(), calls=%async_computation.36 | async-start | bytes 1179648 | tf_op jit(solution)/shard_map/reduce_scatter | solution.py:288
  991.2 316.1 %reduce-scatter.36.cloned.1.call-start = ((), (), s32[]{:S(2)}) async-start(), calls=%async_computation.37 | async-start | bytes 1179648 | tf_op jit(solution)/shard_map/reduce_scatter | solution.py:291
  1142.8 230.1 %reduce-scatter.40.cloned.1.call-start = ((), (), s32[]{:S(2)}) async-start(), calls=%async_computation.39 | async-start | bytes 7077888 | tf_op jit(solution)/shard_map/reduce_scatter | solution.py:297
  1161.0 277.0 %reduce-scatter.42.cloned.1.call-start = ((), (), s32[]{:S(2)}) async-start(), calls=%async_computation.40 | async-start | bytes 7077888 | tf_op jit(solution)/shard_map/reduce_scatter | solution.py:300
  1199.5 303.6 %reduce-scatter.44.cloned.1.call-start = ((), (), s32[]{:S(2)}) async-start(), calls=%async_computation.41 | async-start | bytes 7077888 | tf_op jit(solution)/shard_map/reduce_scatter | solution.py:303
  1238.5 558.9 %all-reduce.27.cloned.1.call-start = ((), (), s32[]{:S(2)}) async-start(), calls=%async_computation.42 | async-start | bytes 16777216 | tf_op jit(solution)/shard_map/psum | solution.py:144
  1375.4 422.1 %copy-start.211 = (f32[256]{0:T(256)S(1)}, f32[256]{0:T(256)}, u32[]{:S(2)}) copy-start(f32[256]{0:T(256)} %copy-done.207) | copy-start | bytes 3076
  (273 other events, 1766.7 us)
Sparse Core Ops, SparseCore 0:
  9.9 26.1 all-gather.13
  37.9 23.3 all-gather.11
  63.2 32.0 all-gather.17
  97.6 23.4 all-gather.29
  122.8 28.0 all-gather.19
  154.4 51.8 all-reduce.24
  214.6 25.4 all-gather.31
  241.9 26.4 all-gather.15
  270.3 22.1 all-gather.27
  294.2 45.3 all-gather.21
  341.5 46.5 all-gather.25
  389.9 45.3 all-gather.23
  451.1 155.0 all-reduce.30
  678.2 120.0 all-reduce.28
  828.7 35.0 reduce-scatter.23
  867.4 35.9 reduce-scatter.15
  906.4 35.9 reduce-scatter.27
  945.5 35.9 reduce-scatter.19
  985.2 35.9 reduce-scatter.17
  1024.2 35.9 reduce-scatter.21
  1063.4 35.9 reduce-scatter.25
  1103.2 35.9 reduce-scatter.29
  1142.5 41.1 reduce-scatter.31
  1186.8 41.0 reduce-scatter.37
  1231.6 35.9 reduce-scatter.33
  1271.3 35.9 reduce-scatter.35
  1311.1 61.7 reduce-scatter.39
  1376.3 61.7 reduce-scatter.41
  1441.5 61.5 reduce-scatter.43
  1506.4 290.9 all-reduce.26
